TPU v7x, 32 devices: a whole 2x2x4 slice. The times are simulated.
32 devices in a mesh: row: 8 (over z, x), col: 4 (over y, core).
Axes of the slice: x: 2, y: 2, z: 4, core: 2. Of those that a mesh axis runs over, the one named last changes fastest.
Arguments:
- tensor: float32 [32, 1024, 1024], P(None, 'row', 'col'), may hold values from -6 to 6
- initial_first: float32 [1024, 256], P('row'), may hold values from -6 to 6
- initial_second: float32 [1024, 256], P('col'), may hold values from -6 to 6
Outputs:
- factor_first: float32 [1024, 256], P('row')
- factor_second: float32 [1024, 256], P('col')
- factor_frames: float32 [32, 256], replicated
- weights: float32 [256], replicated
All inputs are finite; a program needn't handle non-finite values.
Results may differ from a plain program's by a relative error of at most 0.00024.
Values sent between devices are 32-bit elements; how exact they have to be, the bound alone decides.
A program may use at most 128 MiB of HBM per device.

v0:
```python
import math
import jax
import jax.numpy as jnp
from jax import lax
from jax.sharding import PartitionSpec as P

PASSES = 2
epsilon = 1e-06


def solve_gram(partials, hadamard):
    factor_lower = jnp.linalg.cholesky(hadamard)
    midway = lax.linalg.triangular_solve(
        factor_lower, partials, left_side=False, lower=True, transpose_a=True
    )
    return lax.linalg.triangular_solve(
        factor_lower, midway, left_side=False, lower=True, transpose_a=False
    )


def local_gram(matrix):
    return jnp.dot(matrix.T, matrix, precision=lax.Precision.HIGHEST)


def normalize_second(unscaled, row_count):
    squares = lax.psum(jnp.sum(unscaled * unscaled, axis=0), "col")
    scaling = jnp.sqrt(squares / row_count + epsilon)
    normed = unscaled / scaling
    gram_new = lax.psum(local_gram(normed), "col") / row_count
    return (normed, gram_new)


def body(tensor, initial_first, initial_second):
    highest = lax.Precision.HIGHEST
    frames = tensor.shape[0]
    rows_first = tensor.shape[1] * lax.axis_size("row")
    rows_second = tensor.shape[2] * lax.axis_size("col")
    first_gram = lax.psum(local_gram(initial_first), "row") / rows_first
    second = initial_second
    second_gram = lax.psum(local_gram(initial_second), "col") / rows_second
    contracted = jnp.einsum("kij,ir->kjr", tensor, initial_first, precision=highest)
    for repeat in range(PASSES):
        frame_terms = jnp.einsum("kjr,jr->kr", contracted, second, precision=highest)
        frame_sums = lax.psum(frame_terms, ("row", "col"))
        frame_raw = solve_gram(frame_sums, first_gram * second_gram) / math.sqrt(
            rows_first * rows_second
        )
        frame_scaling = jnp.sqrt(jnp.mean(frame_raw * frame_raw, axis=0) + epsilon)
        factor_frames = frame_raw / frame_scaling
        frame_gram = local_gram(factor_frames) / frames
        second_terms = jnp.einsum("kjr,kr->jr", contracted, factor_frames, precision=highest)
        hadamard = first_gram * frame_gram
        own_rows = lax.psum_scatter(second_terms, "row", scatter_dimension=0, tiled=True)
        solved_rows = solve_gram(own_rows, hadamard) / math.sqrt(rows_first * frames)
        second_raw = lax.all_gather(solved_rows, "row", axis=0, tiled=True)
        second, second_gram = normalize_second(second_raw, rows_second)
    second_contracted = jnp.einsum("kij,jr->kir", tensor, second, precision=highest)
    first_terms = jnp.einsum("kir,kr->ir", second_contracted, factor_frames, precision=highest)
    hadamard = second_gram * frame_gram
    own_rows = lax.psum_scatter(first_terms, "col", scatter_dimension=0, tiled=True)
    solved_rows = solve_gram(own_rows, hadamard) / math.sqrt(rows_second * frames)
    first_raw = lax.all_gather(solved_rows, "col", axis=0, tiled=True)
    squares = lax.psum(jnp.sum(first_raw * first_raw, axis=0), "row")
    weights = jnp.sqrt(squares / rows_first + epsilon)
    factor_first = first_raw / weights
    return (factor_first, second, factor_frames, weights)


def solution(mesh):
    placed = (P(None, "row", "col"), P("row", None), P("col", None))
    return jax.shard_map(
        body,
        mesh=mesh,
        in_specs=placed,
        out_specs=(P("row", None), P("col", None), P(), P()),
        check_vma=False,
    )
```

profile of v0, /device:TPU:0, one launch (start us, length us, event | category | flops | bytes accessed | tf_op | source)
XLA Modules:
  0.0 647.6 jit_solution(8311122888523446965)
XLA Ops:
  7.2 2.4 fusion.93
  9.7 1.1 fusion.92
  10.9 10.7 %multiply_reduce_fusion.3 = (f32[256,32]{0,1:T(8,128)S(1)}, f32[32,256,256]{2,1,0:T(8,128)}) fusion(f32[256,256]{0,1:T(8,128)} %bitcast.270, f32[32,128,256]{2,1,0:T(8,128)} %param.8, f32[128,256]{1,0:T(8,128)S(1)} %copy-done), kind=kOutput, calls=%fused_computation.13 | convolution fusion | flops 3225411584 | bytes 13008896 | tf_op jit(solution)/shard_map/kij,ir->kjr/dot_general | solution.py:41
  21.7 43.2 %psum.65 = f32[32,256]{0,1:T(8,128)S(1)} all-reduce(f32[32,256]{0,1:T(8,128)S(1)} %bitcast.276), channel_id=1, replica_groups=mesh['row'=8,'col'=4] {'row','col'}, use_global_device_ids=true, to_apply=%region_6.0 | all-reduce | flops 8192 | bytes 65536 | tf_op jit(solution)/shard_map/psum | solution.py:44
  65.0 55.4 %all-reduce.6.cloned.1.call-done = f32[256,256]{0,1:T(8,128)} async-done(((f32[256,256]{0,1:T(8,128)}), f32[256,256]{0,1:T(8,128)}) %all-reduce.6.cloned.1.call-update) | async-done | bytes 262160 | tf_op jit(solution)/shard_map/psum | solution.py:38
  120.4 1.1 multiply_multiply_fusion.2
  121.7 11.7 %cholesky.256 = f32[128,128]{1,0:T(8,128)S(1)} custom-call(f32[128,128]{1,0:T(8,128)S(1)} %cholesky.422), custom_call_target="Cholesky" | custom-call | tf_op jit(solution)/shard_map/jit(cholesky)/cholesky | solution.py:12
  133.5 9.8 %custom-call.26 = f32[1,128,128]{1,2,0:T(8,128)S(1)} custom-call(f32[1,128,128]{2,1,0:T(8,128)S(1)} %get-tuple-element.150), custom_call_target="InvertDiagBlocksLowerTriangular" | custom-call | tf_op jit(solution)/shard_map/jit(cholesky)/cholesky | solution.py:12
  143.8 11.7 %cholesky.273 = f32[128,128]{1,0:T(8,128)S(1)} custom-call(f32[128,128]{1,0:T(8,128)S(1)} %convolution_subtract_fusion.9), custom_call_target="Cholesky" | custom-call | tf_op jit(solution)/shard_map/jit(cholesky)/cholesky | solution.py:12
  157.6 4.0 while.20
  158.2 1.4 bitcast_dynamic-update-slice_fusion.10
  160.2 1.4 bitcast_dynamic-update-slice_fusion.10
  161.6 20.1 %custom-call.27 = f32[2,128,128]{1,2,0:T(8,128)S(1)} custom-call(f32[2,128,128]{2,1,0:T(8,128)S(1)} %get-tuple-element.71), custom_call_target="InvertDiagBlocksLowerTriangular" | custom-call | tf_op jit(solution)/shard_map/triangular_solve/custom-call.0 | solution.py:13
  183.1 4.9 multiply_reduce_fusion.2
  188.7 11.7 %cholesky.290 = f32[128,128]{1,0:T(8,128)S(1)} custom-call(f32[128,128]{1,0:T(8,128)S(1)} %cholesky.425), custom_call_target="Cholesky" | custom-call | tf_op jit(solution)/shard_map/jit(cholesky)/cholesky | solution.py:12
  200.5 9.8 %custom-call.29 = f32[1,128,128]{1,2,0:T(8,128)S(1)} custom-call(f32[1,128,128]{2,1,0:T(8,128)S(1)} %get-tuple-element.146), custom_call_target="InvertDiagBlocksLowerTriangular" | custom-call | tf_op jit(solution)/shard_map/jit(cholesky)/cholesky | solution.py:12
  210.8 11.7 %cholesky.307 = f32[128,128]{1,0:T(8,128)S(1)} custom-call(f32[128,128]{1,0:T(8,128)S(1)} %convolution_subtract_fusion.7), custom_call_target="Cholesky" | custom-call | tf_op jit(solution)/shard_map/jit(cholesky)/cholesky | solution.py:12
  225.1 4.2 while.21
  225.9 1.4 bitcast_dynamic-update-slice_fusion.11
  227.9 1.4 bitcast_dynamic-update-slice_fusion.11
  229.3 19.7 %custom-call.30 = f32[2,128,128]{1,2,0:T(8,128)S(1)} custom-call(f32[2,128,128]{2,1,0:T(8,128)S(1)} %get-tuple-element.73), custom_call_target="InvertDiagBlocksLowerTriangular" | custom-call | tf_op jit(solution)/shard_map/triangular_solve/custom-call.0 | solution.py:13
  249.0 0.8 reduce-scatter.10.cloned.1.call-done
  250.6 0.9 fusion.54
  252.6 30.9 %all_gather.9 = f32[256,256]{1,0:T(8,128)S(1)} all-gather(f32[32,256]{1,0:T(8,128)S(1)} %maximum_multiply_fusion.1), channel_id=1, replica_groups=mesh['row'=8,'col'=4] {'row'}, dimensions={0}, use_global_device_ids=true | all-gather | bytes 294912 | tf_op jit(solution)/shard_map/all_gather | solution.py:55
  283.5 5.7 psum.66
  289.3 1.3 fusion.14
  290.6 4.2 multiply_reduce_fusion.1
  294.9 39.1 %psum.68 = f32[32,256]{0,1:T(8,128)S(1)} all-reduce(f32[32,256]{0,1:T(8,128)S(1)} %bitcast.277), channel_id=1, replica_groups=mesh['row'=8,'col'=4] {'row','col'}, use_global_device_ids=true, to_apply=%region_12.16 | all-reduce | flops 8192 | bytes 65536 | tf_op jit(solution)/shard_map/psum | solution.py:44
  334.1 1.0 multiply_multiply_fusion.1
  335.3 11.7 %cholesky.324 = f32[128,128]{1,0:T(8,128)S(1)} custom-call(f32[128,128]{1,0:T(8,128)S(1)} %cholesky.428), custom_call_target="Cholesky" | custom-call | tf_op jit(solution)/shard_map/jit(cholesky)/cholesky | solution.py:12
  347.0 9.8 %custom-call.32 = f32[1,128,128]{1,2,0:T(8,128)S(1)} custom-call(f32[1,128,128]{2,1,0:T(8,128)S(1)} %get-tuple-element.142), custom_call_target="InvertDiagBlocksLowerTriangular" | custom-call | tf_op jit(solution)/shard_map/jit(cholesky)/cholesky | solution.py:12
  357.3 11.7 %cholesky.341 = f32[128,128]{1,0:T(8,128)S(1)} custom-call(f32[128,128]{1,0:T(8,128)S(1)} %convolution_subtract_fusion.5), custom_call_target="Cholesky" | custom-call | tf_op jit(solution)/shard_map/jit(cholesky)/cholesky | solution.py:12
  371.7 4.0 while.22
  372.3 1.4 bitcast_dynamic-update-slice_fusion.12
  374.3 1.4 bitcast_dynamic-update-slice_fusion.12
  375.7 20.1 %custom-call.33 = f32[2,128,128]{1,2,0:T(8,128)S(1)} custom-call(f32[2,128,128]{2,1,0:T(8,128)S(1)} %get-tuple-element.75), custom_call_target="InvertDiagBlocksLowerTriangular" | custom-call | tf_op jit(solution)/shard_map/triangular_solve/custom-call.0 | solution.py:13
  397.3 4.9 multiply_reduce_fusion
  402.9 11.7 %cholesky.358 = f32[128,128]{1,0:T(8,128)S(1)} custom-call(f32[128,128]{1,0:T(8,128)S(1)} %cholesky.431), custom_call_target="Cholesky" | custom-call | tf_op jit(solution)/shard_map/jit(cholesky)/cholesky | solution.py:12
  414.7 9.8 %custom-call.35 = f32[1,128,128]{1,2,0:T(8,128)S(1)} custom-call(f32[1,128,128]{2,1,0:T(8,128)S(1)} %get-tuple-element.138), custom_call_target="InvertDiagBlocksLowerTriangular" | custom-call | tf_op jit(solution)/shard_map/jit(cholesky)/cholesky | solution.py:12
  424.9 11.7 %cholesky.375 = f32[128,128]{1,0:T(8,128)S(1)} custom-call(f32[128,128]{1,0:T(8,128)S(1)} %convolution_subtract_fusion.3), custom_call_target="Cholesky" | custom-call | tf_op jit(solution)/shard_map/jit(cholesky)/cholesky | solution.py:12
  439.3 4.2 while.23
  440.1 1.4 bitcast_dynamic-update-slice_fusion.13
  442.1 1.4 bitcast_dynamic-update-slice_fusion.13
  443.5 19.7 %custom-call.36 = f32[2,128,128]{1,2,0:T(8,128)S(1)} custom-call(f32[2,128,128]{2,1,0:T(8,128)S(1)} %get-tuple-element.77), custom_call_target="InvertDiagBlocksLowerTriangular" | custom-call | tf_op jit(solution)/shard_map/triangular_solve/custom-call.0 | solution.py:13
  463.2 2.9 reduce-scatter.12.cloned.1.call-done
  466.9 0.9 fusion.61
  468.9 30.9 %all_gather.10 = f32[256,256]{1,0:T(8,128)S(1)} all-gather(f32[32,256]{1,0:T(8,128)S(1)} %maximum_multiply_fusion.3), channel_id=1, replica_groups=mesh['row'=8,'col'=4] {'row'}, dimensions={0}, use_global_device_ids=true | all-gather | bytes 294912 | tf_op jit(solution)/shard_map/all_gather | solution.py:55
  499.8 5.7 psum.69
  505.5 10.0 %fusion.4 = f32[256,32,128]{2,0,1:T(8,128)} fusion(f32[32,128,256]{2,1,0:T(8,128)} %param.8, f32[256,256]{1,0:T(8,128)S(1)} %broadcast_divide_fusion), kind=kOutput, calls=%fused_computation.40 | convolution fusion | flops 3221225472 | bytes 8650752 | tf_op jit(solution)/shard_map/kij,jr->kir/dot_general | solution.py:57
  515.5 1.3 fusion.94
  516.8 8.2 %fusion = f32[256,1,128]{2,1,0:T(1,128)S(1)} fusion(f32[32,256,1]{0,2,1:T(1,128)S(1)} %copy.67, f32[256,32,128]{2,0,1:T(8,128)} %fusion.4), kind=kOutput, calls=%fused_computation.14 | convolution fusion | flops 12582912 | bytes 4358144 | tf_op jit(solution)/shard_map/kir,kr->ir/dot_general | solution.py:58
  525.0 0.8 copy.73
  525.8 22.6 %all-reduce.12.cloned.1.call-done = f32[256,256]{0,1:T(8,128)} async-done(((f32[256,256]{0,1:T(8,128)}), f32[256,256]{0,1:T(8,128)}) %all-reduce.12.cloned.1.call-update) | async-done | bytes 262160 | tf_op jit(solution)/shard_map/psum | solution.py:29
  548.5 1.0 multiply_multiply_fusion
  549.7 11.7 %cholesky.392 = f32[128,128]{1,0:T(8,128)S(1)} custom-call(f32[128,128]{1,0:T(8,128)S(1)} %cholesky.434), custom_call_target="Cholesky" | custom-call | tf_op jit(solution)/shard_map/jit(cholesky)/cholesky | solution.py:12
  561.4 9.8 %custom-call.38 = f32[1,128,128]{1,2,0:T(8,128)S(1)} custom-call(f32[1,128,128]{2,1,0:T(8,128)S(1)} %get-tuple-element.134), custom_call_target="InvertDiagBlocksLowerTriangular" | custom-call | tf_op jit(solution)/shard_map/jit(cholesky)/cholesky | solution.py:12
  571.7 11.7 %cholesky.409 = f32[128,128]{1,0:T(8,128)S(1)} custom-call(f32[128,128]{1,0:T(8,128)S(1)} %convolution_subtract_fusion.1), custom_call_target="Cholesky" | custom-call | tf_op jit(solution)/shard_map/jit(cholesky)/cholesky | solution.py:12
  586.2 4.0 while.24
  586.8 1.4 bitcast_dynamic-update-slice_fusion.14
  588.8 1.4 bitcast_dynamic-update-slice_fusion.14
  590.2 19.9 %custom-call.39 = f32[2,128,128]{1,2,0:T(8,128)S(1)} custom-call(f32[2,128,128]{2,1,0:T(8,128)S(1)} %get-tuple-element.79), custom_call_target="InvertDiagBlocksLowerTriangular" | custom-call | tf_op jit(solution)/shard_map/triangular_solve/custom-call.0 | solution.py:13
  611.0 0.9 fusion.65
  613.0 5.4 all_gather.11
  618.4 21.4 %psum.71 = f32[256]{0:T(256)S(1)} all-reduce(f32[256]{0:T(256)S(1)} %multiply_reduce_fusion.6), channel_id=1, replica_groups=mesh['row'=8,'col'=4] {'row'}, use_global_device_ids=true, to_apply=%region_20.24 | all-reduce | flops 256 | bytes 2048 | tf_op jit(solution)/shard_map/psum | solution.py:63
  (164 shorter events, 26.6 us)
Async XLA Ops:
  7.2 2.5 copy-start
  7.2 57.8 %all-reduce.8.cloned.1.call-start = ((), (), s32[]{:S(2)}) async-start(), calls=%async_computation.4 | async-start | bytes 524288 | tf_op jit(solution)/shard_map/psum | solution.py:40
  9.6 110.8 %all-reduce.6.cloned.1.call-start = ((), (), s32[]{:S(2)}) async-start(), calls=%async_computation.3 | async-start | bytes 524288 | tf_op jit(solution)/shard_map/psum | solution.py:38
  10.8 239.0 %reduce-scatter.10.cloned.1.call-start = ((), (), s32[]{:S(2)}) async-start(), calls=%async_computation.7 | async-start | bytes 294912
  120.4 67.6 %copy-start.1 = (f32[256,256]{0,1:T(8,128)S(1)}, f32[256,256]{0,1:T(8,128)}, u32[]{:S(2)}) copy-start(f32[256,256]{0,1:T(8,128)} %all-reduce.6.cloned.1.call-done) | copy-start | bytes 786436
  188.0 146.1 %all-reduce.10.cloned.1.call-start = ((), (), s32[]{:S(2)}) async-start(), calls=%async_computation.5 | async-start | bytes 524288 | tf_op jit(solution)/shard_map/psum | solution.py:29
  290.6 175.4 %reduce-scatter.12.cloned.1.call-start = ((), (), s32[]{:S(2)}) async-start(), calls=%async_computation.8 | async-start | bytes 294912
  397.2 118.2 %copy-start.3 = (f32[32,256]{1,0:T(8,128)}, f32[32,256]{1,0:T(8,128)S(1)}, u32[]{:S(2)}) copy-start(f32[32,256]{1,0:T(8,128)S(1)} %fusion.78) | copy-start | bytes 98308
  402.2 146.3 %all-reduce.12.cloned.1.call-start = ((), (), s32[]{:S(2)}) async-start(), calls=%async_computation.6 | async-start | bytes 524288 | tf_op jit(solution)/shard_map/psum | solution.py:29
  505.5 44.2 %copy-start.2 = (f32[256,256]{1,0:T(8,128)}, f32[256,256]{1,0:T(8,128)S(1)}, u32[]{:S(2)}) copy-start(f32[256,256]{1,0:T(8,128)S(1)} %broadcast_divide_fusion) | copy-start | bytes 786436
  516.8 93.4 %reduce-scatter.14.cloned.1.call-start = ((), (), s32[]{:S(2)}) async-start(), calls=%async_computation.9 | async-start | bytes 163840
  639.8 0.7 copy-start.4
Sparse Core Ops, SparseCore 0:
  10.9 34.9 all-reduce.7
  49.3 71.0 all-reduce.5
  188.1 61.6 reduce-scatter.9
  290.7 31.6 all-reduce.9
  402.3 63.6 reduce-scatter.11
  516.9 31.5 all-reduce.11
  551.5 19.8 reduce-scatter.13
where the time goes:
time: 653 us; the launch traced here: 648 us
  other arithmetic  290 us (44%)
  blocking collectives  182 us (28%)
  waiting for transfers between devices  81.9 us (13%)
  matrix products  46.5 us (7%)
  local copies, waits for them, and re-layouts  24.2 us (4%)
  between operations  21.7 us (3%)
    another operation x34, other arithmetic, solve_gram(): factor_lower = jnp.linalg.cholesky(hadamard)  172 us
    another operation x11, other arithmetic, solve_gram(): lax.linalg.triangular_solve(factor_lower, partials, left_side=False, lowe...  99.6 us
    psum x2, blocking collectives, body(): frame_sums = lax.psum(frame_terms, ('row', 'col'))  82.3 us
    all_gather x2, blocking collectives, body(): second_raw = lax.all_gather(solved_rows, 'row', axis=0, tiled=True)  61.7 us
    psum x1, waiting for transfers between devices, body(): first_gram = lax.psum(local_gram(initial_first), 'row') / rows_first  55.4 us
    psum x2, waiting for transfers between devices, normalize_second(): gram_new = lax.psum(local_gram(normed), 'col') / row_count  22.7 us
    another operation x39, local copies, waits for them, and re-layouts, solve_gram(): lax.linalg.triangular_solve(factor_lower, partials, left_side=False, lowe...  22 us
    psum x1, blocking collectives, body(): squares = lax.psum(jnp.sum(first_raw * first_raw, axis=0), 'row')  21.4 us
  transfers between devices with their start and end apart: 7, of which 4 were waited for; matrix products, arithmetic and copies ran while one was open for 32% of the time, Pallas kernels for 0%

commit v1 on v0

--- a/solution.py
+++ b/solution.py
@@ -6,6 +6,25 @@
 
 PASSES = 2
 epsilon = 1e-06
+
+
+def _step_on_roots(tile_in):
+    link_axis = "row"
+    n_parts = lax.axis_size(link_axis)
+    bank = []
+    hop_no = 0
+    while hop_no < n_parts:
+        bank.append((hop_no, (hop_no + 1) % n_parts))
+        hop_no += 1
+    prior = [None] * n_parts
+    prior[n_parts - 1] = tile_in
+    for m in range(n_parts - 2, -1, -1):
+        prior[m] = lax.ppermute(prior[m + 1], axis_name=link_axis, perm=bank)
+    tmp = jnp.concatenate(prior, axis=0)
+    arr_next = lax.axis_index(link_axis)
+    x_next = (arr_next + 1) * tile_in.shape[0]
+    formed = jnp.roll(tmp, x_next, axis=0)
+    return formed
 
 
 def solve_gram(partials, hadamard):
@@ -52,7 +71,7 @@
         hadamard = first_gram * frame_gram
         own_rows = lax.psum_scatter(second_terms, "row", scatter_dimension=0, tiled=True)
         solved_rows = solve_gram(own_rows, hadamard) / math.sqrt(rows_first * frames)
-        second_raw = lax.all_gather(solved_rows, "row", axis=0, tiled=True)
+        second_raw = _step_on_roots(solved_rows)
         second, second_gram = normalize_second(second_raw, rows_second)
     second_contracted = jnp.einsum("kij,jr->kir", tensor, second, precision=highest)
     first_terms = jnp.einsum("kir,kr->ir", second_contracted, factor_frames, precision=highest)

time: 653 us -> 683 us (1.046)
  waiting for transfers between devices: 81.9 us -> 171 us
  blocking collectives: 182 us -> 119 us
    ppermute x0 -> x14, waiting for transfers between devices: none -> 90.1 us  [_step_on_roots(): prior[m] = lax.ppermute(prior[m + 1], axis_name=link_axis, perm=bank)]
    all_gather x2 -> x0, blocking collectives: 61.7 us -> none  [body(): second_raw = lax.all_gather(solved_rows, 'row', axis=0, tiled=True)]
  transfers between devices with their start and end apart: 7 -> 21, of which waited for: 4 -> 18; matrix products, arithmetic and copies ran while one was open for 32% -> 30% of each run, Pallas kernels for 0% -> 0%
where the time goes in v1:
time: 683 us; the launch traced here: 678 us
  other arithmetic  290 us (42%)
  waiting for transfers between devices  171 us (25%)
  blocking collectives  119 us (17%)
  matrix products  46.5 us (7%)
  local copies, waits for them, and re-layouts  24.2 us (4%)
  between operations  21.8 us (3%)
    another operation x34, other arithmetic, solve_gram(): factor_lower = jnp.linalg.cholesky(hadamard)  172 us
    another operation x11, other arithmetic, solve_gram(): lax.linalg.triangular_solve(factor_lower, partials, left_side=False, lowe...  99.6 us
    ppermute x14, waiting for transfers between devices, _step_on_roots(): prior[m] = lax.ppermute(prior[m + 1], axis_name=link_axis, perm=bank)  90.1 us
    psum x2, blocking collectives, body(): frame_sums = lax.psum(frame_terms, ('row', 'col'))  81.2 us
    psum x1, waiting for transfers between devices, body(): first_gram = lax.psum(local_gram(initial_first), 'row') / rows_first  55.4 us
    another operation x39, local copies, waits for them, and re-layouts, solve_gram(): lax.linalg.triangular_solve(factor_lower, partials, left_side=False, lowe...  22 us
    psum x1, blocking collectives, body(): squares = lax.psum(jnp.sum(first_raw * first_raw, axis=0), 'row')  21.4 us
    psum x2, waiting for transfers between devices, normalize_second(): gram_new = lax.psum(local_gram(normed), 'col') / row_count  21 us
  transfers between devices with their start and end apart: 21, of which 18 were waited for; matrix products, arithmetic and copies ran while one was open for 30% of the time, Pallas kernels for 0%

profile of v1, /device:TPU:0, one launch (start us, length us, event | category | flops | bytes accessed | tf_op | source)
XLA Modules:
  0.0 677.5 jit_solution(12458868012284297999)
XLA Ops:
  7.2 2.4 fusion.96
  10.9 10.7 %multiply_reduce_fusion.3 = (f32[256,32]{0,1:T(8,128)S(1)}, f32[32,256,256]{2,1,0:T(8,128)}) fusion(f32[256,256]{0,1:T(8,128)} %bitcast.270, f32[32,128,256]{2,1,0:T(8,128)} %param.10, f32[128,256]{1,0:T(8,128)S(1)} %copy-done), kind=kOutput, calls=%fused_computation.13 | convolution fusion | flops 3225411584 | bytes 13008896 | tf_op jit(solution)/shard_map/kij,ir->kjr/dot_general | solution.py:60
  21.7 43.2 %psum.65 = f32[32,256]{0,1:T(8,128)S(1)} all-reduce(f32[32,256]{0,1:T(8,128)S(1)} %bitcast.276), channel_id=1, replica_groups=mesh['row'=8,'col'=4] {'row','col'}, use_global_device_ids=true, to_apply=%region_6.8 | all-reduce | flops 8192 | bytes 65536 | tf_op jit(solution)/shard_map/psum | solution.py:63
  65.0 55.4 %all-reduce.6.cloned.1.call-done = f32[256,256]{0,1:T(8,128)} async-done(((f32[256,256]{0,1:T(8,128)}), f32[256,256]{0,1:T(8,128)}) %all-reduce.6.cloned.1.call-update) | async-done | bytes 262160 | tf_op jit(solution)/shard_map/psum | solution.py:57
  121.7 11.7 %cholesky.256 = f32[128,128]{1,0:T(8,128)S(1)} custom-call(f32[128,128]{1,0:T(8,128)S(1)} %cholesky.422), custom_call_target="Cholesky" | custom-call | tf_op jit(solution)/shard_map/jit(cholesky)/cholesky | solution.py:31
  133.5 9.8 %custom-call.26 = f32[1,128,128]{1,2,0:T(8,128)S(1)} custom-call(f32[1,128,128]{2,1,0:T(8,128)S(1)} %get-tuple-element.153), custom_call_target="InvertDiagBlocksLowerTriangular" | custom-call | tf_op jit(solution)/shard_map/jit(cholesky)/cholesky | solution.py:31
  143.8 11.7 %cholesky.273 = f32[128,128]{1,0:T(8,128)S(1)} custom-call(f32[128,128]{1,0:T(8,128)S(1)} %convolution_subtract_fusion.9), custom_call_target="Cholesky" | custom-call | tf_op jit(solution)/shard_map/jit(cholesky)/cholesky | solution.py:31
  157.6 4.0 while.20
  158.2 1.4 bitcast_dynamic-update-slice_fusion.10
  160.2 1.4 bitcast_dynamic-update-slice_fusion.10
  161.6 20.1 %custom-call.27 = f32[2,128,128]{1,2,0:T(8,128)S(1)} custom-call(f32[2,128,128]{2,1,0:T(8,128)S(1)} %get-tuple-element.72), custom_call_target="InvertDiagBlocksLowerTriangular" | custom-call | tf_op jit(solution)/shard_map/triangular_solve/custom-call.0 | solution.py:32
  183.1 4.9 multiply_reduce_fusion.2
  188.7 11.7 %cholesky.290 = f32[128,128]{1,0:T(8,128)S(1)} custom-call(f32[128,128]{1,0:T(8,128)S(1)} %cholesky.425), custom_call_target="Cholesky" | custom-call | tf_op jit(solution)/shard_map/jit(cholesky)/cholesky | solution.py:31
  200.5 9.8 %custom-call.29 = f32[1,128,128]{1,2,0:T(8,128)S(1)} custom-call(f32[1,128,128]{2,1,0:T(8,128)S(1)} %get-tuple-element.149), custom_call_target="InvertDiagBlocksLowerTriangular" | custom-call | tf_op jit(solution)/shard_map/jit(cholesky)/cholesky | solution.py:31
  210.8 11.7 %cholesky.307 = f32[128,128]{1,0:T(8,128)S(1)} custom-call(f32[128,128]{1,0:T(8,128)S(1)} %convolution_subtract_fusion.7), custom_call_target="Cholesky" | custom-call | tf_op jit(solution)/shard_map/jit(cholesky)/cholesky | solution.py:31
  225.1 4.2 while.21
  225.9 1.4 bitcast_dynamic-update-slice_fusion.11
  227.9 1.4 bitcast_dynamic-update-slice_fusion.11
  229.3 19.7 %custom-call.30 = f32[2,128,128]{1,2,0:T(8,128)S(1)} custom-call(f32[2,128,128]{2,1,0:T(8,128)S(1)} %get-tuple-element.74), custom_call_target="InvertDiagBlocksLowerTriangular" | custom-call | tf_op jit(solution)/shard_map/triangular_solve/custom-call.0 | solution.py:32
  252.6 1.5 collective-permute-start
  254.1 5.2 collective-permute-done
  259.3 6.6 collective-permute-done.1
  265.9 6.8 %collective-permute-done.2 = f32[32,256]{1,0:T(8,128)S(1)} collective-permute-done((f32[32,256]{1,0:T(8,128)S(1)}, f32[32,256]{1,0:T(8,128)S(1)}, u32[]{:S(2)}, u32[]{:S(2)}) %collective-permute-start.2) | collective-permute-done | bytes 32800 | tf_op jit(solution)/shard_map/ppermute | solution.py:22
  272.8 6.6 collective-permute-done.3
  279.4 6.6 collective-permute-done.4
  286.0 6.6 collective-permute-done.5
  292.6 6.6 collective-permute-done.6
  299.4 5.7 psum.66
  306.5 4.2 multiply_reduce_fusion.1
  310.9 38.0 %psum.68 = f32[32,256]{0,1:T(8,128)S(1)} all-reduce(f32[32,256]{0,1:T(8,128)S(1)} %bitcast.277), channel_id=1, replica_groups=mesh['row'=8,'col'=4] {'row','col'}, use_global_device_ids=true, to_apply=%region_12.0 | all-reduce | flops 8192 | bytes 65536 | tf_op jit(solution)/shard_map/psum | solution.py:63
  350.1 11.7 %cholesky.324 = f32[128,128]{1,0:T(8,128)S(1)} custom-call(f32[128,128]{1,0:T(8,128)S(1)} %cholesky.428), custom_call_target="Cholesky" | custom-call | tf_op jit(solution)/shard_map/jit(cholesky)/cholesky | solution.py:31
  361.9 9.8 %custom-call.32 = f32[1,128,128]{1,2,0:T(8,128)S(1)} custom-call(f32[1,128,128]{2,1,0:T(8,128)S(1)} %get-tuple-element.145), custom_call_target="InvertDiagBlocksLowerTriangular" | custom-call | tf_op jit(solution)/shard_map/jit(cholesky)/cholesky | solution.py:31
  372.1 11.7 %cholesky.341 = f32[128,128]{1,0:T(8,128)S(1)} custom-call(f32[128,128]{1,0:T(8,128)S(1)} %convolution_subtract_fusion.5), custom_call_target="Cholesky" | custom-call | tf_op jit(solution)/shard_map/jit(cholesky)/cholesky | solution.py:31
  386.5 4.0 while.22
  387.1 1.4 bitcast_dynamic-update-slice_fusion.12
  389.1 1.4 bitcast_dynamic-update-slice_fusion.12
  390.5 20.1 %custom-call.33 = f32[2,128,128]{1,2,0:T(8,128)S(1)} custom-call(f32[2,128,128]{2,1,0:T(8,128)S(1)} %get-tuple-element.76), custom_call_target="InvertDiagBlocksLowerTriangular" | custom-call | tf_op jit(solution)/shard_map/triangular_solve/custom-call.0 | solution.py:32
  412.1 4.9 multiply_reduce_fusion
  417.6 11.7 %cholesky.358 = f32[128,128]{1,0:T(8,128)S(1)} custom-call(f32[128,128]{1,0:T(8,128)S(1)} %cholesky.431), custom_call_target="Cholesky" | custom-call | tf_op jit(solution)/shard_map/jit(cholesky)/cholesky | solution.py:31
  429.4 9.8 %custom-call.35 = f32[1,128,128]{1,2,0:T(8,128)S(1)} custom-call(f32[1,128,128]{2,1,0:T(8,128)S(1)} %get-tuple-element.141), custom_call_target="InvertDiagBlocksLowerTriangular" | custom-call | tf_op jit(solution)/shard_map/jit(cholesky)/cholesky | solution.py:31
  439.7 11.7 %cholesky.375 = f32[128,128]{1,0:T(8,128)S(1)} custom-call(f32[128,128]{1,0:T(8,128)S(1)} %convolution_subtract_fusion.3), custom_call_target="Cholesky" | custom-call | tf_op jit(solution)/shard_map/jit(cholesky)/cholesky | solution.py:31
  454.1 4.2 while.23
  454.8 1.4 bitcast_dynamic-update-slice_fusion.13
  458.2 19.7 %custom-call.36 = f32[2,128,128]{1,2,0:T(8,128)S(1)} custom-call(f32[2,128,128]{2,1,0:T(8,128)S(1)} %get-tuple-element.78), custom_call_target="InvertDiagBlocksLowerTriangular" | custom-call | tf_op jit(solution)/shard_map/triangular_solve/custom-call.0 | solution.py:32
  477.9 3.9 reduce-scatter.12.cloned.1.call-done
  484.6 1.5 collective-permute-start.7
  486.1 5.2 collective-permute-done.7
  491.3 6.6 collective-permute-done.8
  497.9 6.8 %collective-permute-done.9 = f32[32,256]{1,0:T(8,128)S(1)} collective-permute-done((f32[32,256]{1,0:T(8,128)S(1)}, f32[32,256]{1,0:T(8,128)S(1)}, u32[]{:S(2)}, u32[]{:S(2)}) %collective-permute-start.9) | collective-permute-done | bytes 32800 | tf_op jit(solution)/shard_map/ppermute | solution.py:22
  504.8 6.6 collective-permute-done.10
  511.4 6.6 collective-permute-done.11
  518.0 6.6 collective-permute-done.12
  524.7 6.5 collective-permute-done.13
  531.4 5.7 psum.69
  537.2 10.0 %fusion.6 = f32[256,32,128]{2,0,1:T(8,128)} fusion(f32[32,128,256]{2,1,0:T(8,128)} %param.10, f32[256,256]{1,0:T(8,128)S(1)} %broadcast_divide_fusion), kind=kOutput, calls=%fused_computation.46 | convolution fusion | flops 3221225472 | bytes 8650752 | tf_op jit(solution)/shard_map/kij,jr->kir/dot_general | solution.py:76
  548.5 8.2 %fusion = f32[256,1,128]{2,1,0:T(1,128)S(1)} fusion(f32[32,256,1]{0,2,1:T(1,128)S(1)} %copy.67, f32[256,32,128]{2,0,1:T(8,128)} %fusion.6), kind=kOutput, calls=%fused_computation.14 | convolution fusion | flops 12582912 | bytes 4358144 | tf_op jit(solution)/shard_map/kir,kr->ir/dot_general | solution.py:77
  557.5 20.9 %all-reduce.12.cloned.1.call-done = f32[256,256]{0,1:T(8,128)} async-done(((f32[256,256]{0,1:T(8,128)}), f32[256,256]{0,1:T(8,128)}) %all-reduce.12.cloned.1.call-update) | async-done | bytes 262160 | tf_op jit(solution)/shard_map/psum | solution.py:48
  579.6 11.7 %cholesky.392 = f32[128,128]{1,0:T(8,128)S(1)} custom-call(f32[128,128]{1,0:T(8,128)S(1)} %cholesky.434), custom_call_target="Cholesky" | custom-call | tf_op jit(solution)/shard_map/jit(cholesky)/cholesky | solution.py:31
  591.4 9.8 %custom-call.38 = f32[1,128,128]{1,2,0:T(8,128)S(1)} custom-call(f32[1,128,128]{2,1,0:T(8,128)S(1)} %get-tuple-element.137), custom_call_target="InvertDiagBlocksLowerTriangular" | custom-call | tf_op jit(solution)/shard_map/jit(cholesky)/cholesky | solution.py:31
  601.7 11.7 %cholesky.409 = f32[128,128]{1,0:T(8,128)S(1)} custom-call(f32[128,128]{1,0:T(8,128)S(1)} %convolution_subtract_fusion.1), custom_call_target="Cholesky" | custom-call | tf_op jit(solution)/shard_map/jit(cholesky)/cholesky | solution.py:31
  616.1 4.0 while.24
  620.1 19.9 %custom-call.39 = f32[2,128,128]{1,2,0:T(8,128)S(1)} custom-call(f32[2,128,128]{2,1,0:T(8,128)S(1)} %get-tuple-element.80), custom_call_target="InvertDiagBlocksLowerTriangular" | custom-call | tf_op jit(solution)/shard_map/triangular_solve/custom-call.0 | solution.py:32
  642.9 5.4 all_gather.3
  648.4 21.4 %psum.71 = f32[256]{0:T(256)S(1)} all-reduce(f32[256]{0:T(256)S(1)} %multiply_reduce_fusion.6), channel_id=1, replica_groups=mesh['row'=8,'col'=4] {'row'}, use_global_device_ids=true, to_apply=%region_20.25 | all-reduce | flops 256 | bytes 2048 | tf_op jit(solution)/shard_map/psum | solution.py:82
  (206 shorter events, 42.0 us)
Async XLA Ops:
  7.2 2.5 copy-start
  7.2 57.8 %all-reduce.8.cloned.1.call-start = ((), (), s32[]{:S(2)}) async-start(), calls=%async_computation.4 | async-start | bytes 524288 | tf_op jit(solution)/shard_map/psum | solution.py:59
  9.6 110.8 %all-reduce.6.cloned.1.call-start = ((), (), s32[]{:S(2)}) async-start(), calls=%async_computation.3 | async-start | bytes 524288 | tf_op jit(solution)/shard_map/psum | solution.py:57
  10.8 239.0 %reduce-scatter.10.cloned.1.call-start = ((), (), s32[]{:S(2)}) async-start(), calls=%async_computation.7 | async-start | bytes 294912
  120.4 67.6 %copy-start.1 = (f32[256,256]{0,1:T(8,128)S(1)}, f32[256,256]{0,1:T(8,128)}, u32[]{:S(2)}) copy-start(f32[256,256]{0,1:T(8,128)} %all-reduce.6.cloned.1.call-done) | copy-start | bytes 786436
  188.0 160.9 %all-reduce.10.cloned.1.call-start = ((), (), s32[]{:S(2)}) async-start(), calls=%async_computation.5 | async-start | bytes 524288 | tf_op jit(solution)/shard_map/psum | solution.py:48
  252.6 6.7 collective-permute-start
  259.3 6.6 collective-permute-start.1
  265.9 6.9 %collective-permute-start.2 = (f32[32,256]{1,0:T(8,128)S(1)}, f32[32,256]{1,0:T(8,128)S(1)}, u32[]{:S(2)}, u32[]{:S(2)}) collective-permute-start(f32[32,256]{1,0:T(8,128)S(1)} %collective-permute-done.1), channel_id=1, source_target_pairs={{0,4},{4,8},{8,12},{12,16},{16,20},{20,24},{24,28},{28,0},{1,5},{5... | collective-permute-start | bytes 98312 | tf_op jit(solution)/shard_map/ppermute | solution.py:22
  272.8 6.6 collective-permute-start.3
  279.4 6.6 collective-permute-start.4
  286.0 6.6 collective-permute-start.5
  292.6 6.6 collective-permute-start.6
  306.5 175.4 %reduce-scatter.12.cloned.1.call-start = ((), (), s32[]{:S(2)}) async-start(), calls=%async_computation.8 | async-start | bytes 294912
  412.0 135.1 %copy-start.3 = (f32[32,256]{1,0:T(8,128)}, f32[32,256]{1,0:T(8,128)S(1)}, u32[]{:S(2)}) copy-start(f32[32,256]{1,0:T(8,128)S(1)} %fusion.80) | copy-start | bytes 98308
  416.9 161.5 %all-reduce.12.cloned.1.call-start = ((), (), s32[]{:S(2)}) async-start(), calls=%async_computation.6 | async-start | bytes 524288 | tf_op jit(solution)/shard_map/psum | solution.py:48
  484.6 6.7 collective-permute-start.7
  491.3 6.6 collective-permute-start.8
  497.9 6.8 %collective-permute-start.9 = (f32[32,256]{1,0:T(8,128)S(1)}, f32[32,256]{1,0:T(8,128)S(1)}, u32[]{:S(2)}, u32[]{:S(2)}) collective-permute-start(f32[32,256]{1,0:T(8,128)S(1)} %collective-permute-done.8), channel_id=1, source_target_pairs={{0,4},{4,8},{8,12},{12,16},{16,20},{20,24},{24,28},{28,0},{1,5},{5... | collective-permute-start | bytes 98312 | tf_op jit(solution)/shard_map/ppermute | solution.py:22
  504.7 6.6 collective-permute-start.10
  511.4 6.6 collective-permute-start.11
  518.0 6.6 collective-permute-start.12
  524.6 6.6 collective-permute-start.13
  537.2 42.4 %copy-start.2 = (f32[256,256]{1,0:T(8,128)}, f32[256,256]{1,0:T(8,128)S(1)}, u32[]{:S(2)}) copy-start(f32[256,256]{1,0:T(8,128)S(1)} %broadcast_divide_fusion) | copy-start | bytes 786436
  548.5 91.6 %reduce-scatter.14.cloned.1.call-start = ((), (), s32[]{:S(2)}) async-start(), calls=%async_computation.9 | async-start | bytes 163840
  669.7 0.7 copy-start.4
Sparse Core Ops, SparseCore 0:
  10.9 34.9 all-reduce.7
  49.3 71.0 all-reduce.5
  188.1 61.6 reduce-scatter.9
  306.6 29.9 all-reduce.9
  417.0 64.7 reduce-scatter.11
  548.6 29.8 all-reduce.11
  581.4 19.8 reduce-scatter.13
